TPU v7x, 256 devices: a 8x8x2 block of a 8x8x16 slice. The times are simulated.
256 devices in a mesh: sims: 2 (over z), rows: 16 (over y, core), fields: 8 (over x).
Axes of the slice: x: 8, y: 8, z: 2, core: 2. Of those that a mesh axis runs over, the one named last changes fastest.
The devices are a block of a 8x8x16 slice.
Arguments:
- sky_maps: float32 [6, 256, 16384], P('sims', 'rows', 'fields'), parts along dimension 0, may hold values from -7 to 7
- band_cuts: int32 [6], replicated, may hold values from 1 to 8191, as said below
- filters: float32 [3, 256, 16384], P(None, ('rows', 'fields')), may hold values from 0.3 to 3
- wiener: float32 [2, 256, 16384], P(None, ('rows', 'fields')), may hold values from 0.3 to 3
- response: float32 [256, 16384], P(('rows', 'fields')), may hold values from 0.5 to 2
Outputs:
- phi_curl: float32 [4, 256, 16384], P('sims', 'rows', 'fields'), parts along dimension 0
There are 2 independent parts, one for each index of `sims`. A program takes and returns all parts, laid end to end along the dimension named above; an argument that names none is the same for every part. Nothing has to cross between parts.
Inputs may be any that keep to these rules, and one draw needn't show every extreme that they name: `band_cuts`: entries 0, 2 and 4 are the smallest multipole indices of the temperature, polarization and estimate bands and lie below 512; entries 1, 3 and 5 are the largest and are at least 4096.
All inputs are finite; a program needn't handle non-finite values.
Results may differ from a plain program's by a relative error of at most 0.00019.
Values sent between devices are 32-bit elements; how exact they have to be, the bound alone decides.
A program may use at most 128 MiB of HBM per device.

v0:
```python
import functools
import math

import jax
import jax.numpy as jnp
import numpy as np
from jax import lax
from jax.experimental import pallas as pl
from jax.experimental.pallas import tpu as pltpu
from jax.sharding import PartitionSpec as P

MESH = pl.DeviceIdType.MESH
F32 = jnp.float32
BF16 = jnp.bfloat16


def halves(table):
    high = table.astype(np.float32).astype(BF16)
    low = (table - high.astype(np.float64)).astype(np.float32).astype(BF16)
    return np.stack([np.asarray(high), np.asarray(low)])


def phases(left, right, period):
    angles = 2.0 * math.pi / period * (left[:, None] * right[None, :] % period)
    return np.cos(angles), np.sin(angles)


def tables(rows, fields, local, width):
    groups = rows * fields
    total = groups * local
    length = groups * width
    cos, sin = phases(np.arange(total), np.arange(total), total)
    forward = np.stack([np.concatenate([cos, sin], 1), np.concatenate([-sin, cos], 1)])
    forward = forward.reshape(2, groups, local, 2 * total).transpose(1, 0, 2, 3)
    along_rows = halves(forward.reshape(2 * total, 2 * total))
    place = np.arange(groups)
    block = place % fields * rows + place // fields
    cos, sin = phases(np.arange(groups), block, groups)
    same = np.eye(local)
    signed = np.stack([np.stack([cos, sin]), np.stack([-sin, cos])])
    mixed = np.einsum("cdkp,ij->cikpdj", signed, same)
    across = halves(mixed.reshape(2 * total, 2 * total))
    cos, sin = phases(np.arange(width), np.arange(width), width)
    inner = np.einsum("tcq,ij->ictqj", np.stack([cos, sin]), same)
    within = halves(inner.reshape(local * width, 2 * width * local))
    cos, sin = phases(np.arange(groups), np.arange(width), length)
    twiddle = np.stack([cos, sin]).astype(np.float32)
    return along_rows, across, within, twiddle


def dot(left, right):
    return jnp.dot(left, right, preferred_element_type=F32)


def split(value):
    high = value.astype(BF16)
    return high, (value - high.astype(F32)).astype(BF16)


def table_dot(table, value):
    high, low = split(value)
    return dot(table[0], high) + dot(table[0], low) + dot(table[1], high)


def dot_table(value, table):
    high, low = split(value)
    return dot(high, table[0]) + dot(low, table[0]) + dot(high, table[1])


def kernel(
    sizes,
    cuts,
    sky_hbm,
    filters_hbm,
    wiener_hbm,
    response_hbm,
    rows_hbm,
    across_hbm,
    within_hbm,
    twiddle_hbm,
    out_hbm,
    sky,
    raw,
    fwd_rows,
    inv_rows,
    fwd_across,
    inv_across,
    fwd_within,
    inv_within,
    twiddle,
    weights,
    sent,
    held,
    result,
    send_sems,
    recv_sems,
    load_sems,
):
    n_rows, n_fields, local, width = sizes
    groups = n_rows * n_fields
    total = groups * local
    length = groups * width
    slab = total // n_rows
    lines = 2 * local
    row_me = lax.axis_index("rows")
    field_me = lax.axis_index("fields")
    me = row_me * n_fields + field_me

    def peer(step):
        return lax.rem(row_me + step // n_fields, n_rows), lax.rem(
            field_me + lax.rem(step, n_fields), n_fields
        )

    barrier = pltpu.get_barrier_semaphore()

    def greet(step, carry):
        row, field = peer(step)
        pl.semaphore_signal(
            barrier, inc=1, device_id={"rows": row, "fields": field}, device_id_type=MESH
        )
        return carry

    lax.fori_loop(1, groups, greet, 0)

    loads = [
        pltpu.make_async_copy(source, target, load_sems.at[i])
        for i, (source, target) in enumerate(
            [
                (rows_hbm, fwd_rows),
                (across_hbm, fwd_across),
                (within_hbm, fwd_within),
                (twiddle_hbm, twiddle),
                (filters_hbm, raw.at[0:3]),
                (wiener_hbm, raw.at[3:5]),
                (response_hbm, raw.at[5:6]),
            ]
        )
    ]
    for load in loads:
        load.start()
    pl.semaphore_wait(barrier, groups - 1)

    for i in range(3):

        def scatter(step, carry, i=i):
            row = lax.rem(row_me + step, n_rows)
            pltpu.make_async_remote_copy(
                src_ref=sky_hbm.at[i, :, pl.ds(pl.multiple_of(row * width, width), width)],
                dst_ref=sky.at[i, pl.ds(row_me * slab, slab), :],
                send_sem=send_sems.at[i],
                recv_sem=recv_sems.at[i],
                device_id={"rows": row},
                device_id_type=MESH,
            ).start()
            return carry

        lax.fori_loop(1, n_rows, scatter, 0)
        pltpu.make_async_copy(
            sky_hbm.at[i, :, pl.ds(pl.multiple_of(row_me * width, width), width)],
            sky.at[i, pl.ds(row_me * slab, slab), :],
            recv_sems.at[i],
        ).start()

    def exchange(slot):
        def hand(step, carry):
            row, field = peer(step)
            pltpu.make_async_remote_copy(
                src_ref=sent.at[slot, pl.ds((row * n_fields + field) * lines, lines), :],
                dst_ref=held.at[slot, pl.ds(me * lines, lines), :],
                send_sem=send_sems.at[3 + slot],
                recv_sem=recv_sems.at[3 + slot],
                device_id={"rows": row, "fields": field},
                device_id_type=MESH,
            ).start()
            return carry

        lax.fori_loop(1, groups, hand, 0)
        pltpu.make_async_copy(
            sent.at[slot, pl.ds(me * lines, lines), :],
            held.at[slot, pl.ds(me * lines, lines), :],
            recv_sems.at[3 + slot],
        ).start()

    def arrive(slot):
        pltpu.make_async_copy(held.at[slot], held.at[slot], recv_sems.at[3 + slot]).wait()
        return held[slot]

    for load in loads:
        load.wait()
    for i in range(2):
        inv_rows[i] = fwd_rows[i].T
        inv_across[i] = fwd_across[i].T
        for t in range(2):
            span = slice(t * local * width, (t + 1) * local * width)
            inv_within[i, :, span] = fwd_within[i, :, span].T

    shape = (groups, width * local)
    k = lax.broadcasted_iota(jnp.int32, shape, 0)
    lane = lax.broadcasted_iota(jnp.int32, shape, 1)
    kx = groups * (lane // local) + k
    kx = jnp.where(kx < length // 2, kx, kx - length)
    ky = local * me + lane % local
    ky = jnp.where(ky < total // 2, ky, ky - total)
    sy = (length // total) * ky
    k2 = kx * kx + sy * sy

    def band(i):
        low, high = cuts[2 * i], cuts[2 * i + 1]
        return jnp.where((k2 >= low * low) & (k2 <= high * high), 1.0, 0.0).astype(F32)

    floor = jnp.maximum(k2, 1).astype(F32)
    cos_two = (kx * kx - sy * sy).astype(F32) / floor
    sin_two = (2 * kx * sy).astype(F32) / floor
    ux = (2 * kx).astype(F32) / length
    uy = (2 * ky).astype(F32) / total
    norm = 1.0 / (length * total)
    weights[0] = band(0) * raw[0].T * norm
    weights[1] = raw[3].T
    band_pol = band(1)
    weights[2] = band_pol * raw[1].T * norm
    weights[3] = band_pol * raw[2].T * norm
    weights[4] = raw[4].T
    out_weight = band(2) * raw[5].T * norm
    weights[5] = out_weight * uy
    weights[6] = out_weight * ux
    weights[7] = cos_two
    weights[8] = sin_two
    weights[9] = ux
    weights[10] = uy

    def sides(value):
        return jnp.concatenate([value] * local, axis=1)

    def columns_forward(value):
        mixed = table_dot(fwd_across, value)
        parts = [mixed[i * groups : (i + 1) * groups] for i in range(lines)]
        real = jnp.concatenate(parts[:local], axis=1)
        imag = jnp.concatenate(parts[local:], axis=1)
        cos, sin = sides(twiddle[0]), sides(twiddle[1])
        turned = jnp.concatenate([real * cos + imag * sin, imag * cos - real * sin], axis=0)
        out = dot_table(turned, fwd_within)
        half = width * local
        return (
            out[:groups, :half] + out[groups:, half:],
            out[groups:, :half] - out[:groups, half:],
        )

    def columns_inverse(real, imag):
        out = dot_table(jnp.concatenate([real, imag], axis=0), inv_within)
        half = width * local
        real = out[:groups, :half] - out[groups:, half:]
        imag = out[groups:, :half] + out[:groups, half:]
        cos, sin = sides(twiddle[0]), sides(twiddle[1])
        real, imag = real * cos - imag * sin, imag * cos + real * sin
        parts = [
            part[:, i * width : (i + 1) * width] for part in (real, imag) for i in range(local)
        ]
        return table_dot(inv_across, jnp.concatenate(parts, axis=0))

    for i in range(3):
        pltpu.make_async_copy(sky.at[i], sky.at[i], recv_sems.at[i]).wait()
        high, low = split(sky[i])
        sent[i] = (
            dot(fwd_rows[0, :, :total], high)
            + dot(fwd_rows[0, :, :total], low)
            + dot(fwd_rows[1, :, :total], high)
        )
        exchange(i)

    def leg(slot, real, imag):
        sent[slot] = columns_inverse(real, imag)
        exchange(slot)

    t_real, t_imag = columns_forward(arrive(0))
    t_real, t_imag = weights[0] * t_real, weights[0] * t_imag
    leg(3, t_real, t_imag)
    w_real, w_imag = weights[1] * t_real, weights[1] * t_imag
    ux, uy = weights[9], weights[10]
    leg(4, -uy * w_real - ux * w_imag, ux * w_real - uy * w_imag)
    q_real, q_imag = columns_forward(arrive(1))
    u_real, u_imag = columns_forward(arrive(2))
    cos_two, sin_two = weights[7], weights[8]
    e_real = -weights[2] * (cos_two * q_real + sin_two * u_real)
    e_imag = -weights[2] * (cos_two * q_imag + sin_two * u_imag)
    b_real = weights[3] * (sin_two * q_real - cos_two * u_real)
    b_imag = weights[3] * (sin_two * q_imag - cos_two * u_imag)
    s_real, s_imag = e_real - b_imag, e_imag + b_real
    leg(5, sin_two * s_imag - cos_two * s_real, -cos_two * s_imag - sin_two * s_real)
    w_real, w_imag = weights[4] * e_real, weights[4] * e_imag
    w_real, w_imag = sin_two * w_imag - cos_two * w_real, -cos_two * w_imag - sin_two * w_real
    leg(6, -uy * w_real - ux * w_imag, ux * w_real - uy * w_imag)
    leg(7, uy * w_real - ux * w_imag, ux * w_real + uy * w_imag)

    def to_maps(slot):
        maps = table_dot(inv_rows, arrive(slot))
        return maps[:total], maps[total:]

    a_real, a_imag = to_maps(3)
    g_real, g_imag = to_maps(4)
    c_real = a_real * g_real - a_imag * g_imag
    c_imag = a_real * g_imag + a_imag * g_real
    p_real, p_imag = to_maps(5)
    h_real, h_imag = to_maps(6)
    c_real = c_real + 0.5 * (p_real * h_real + p_imag * h_imag)
    c_imag = c_imag + 0.5 * (p_real * h_imag - p_imag * h_real)
    h_real, h_imag = to_maps(7)
    c_real = c_real + 0.5 * (p_real * h_real + p_imag * h_imag)
    c_imag = c_imag + 0.5 * (p_imag * h_real - p_real * h_imag)
    sent[8] = table_dot(fwd_rows, jnp.concatenate([c_real, c_imag], axis=0))
    exchange(8)
    c_real, c_imag = columns_forward(arrive(8))
    leg(9, weights[5] * c_real - weights[6] * c_imag, weights[6] * c_real + weights[5] * c_imag)
    e_real, e_imag = to_maps(9)
    result[0] = e_real
    result[1] = e_imag

    def gather(step, carry):
        row = lax.rem(row_me + step, n_rows)
        pltpu.make_async_remote_copy(
            src_ref=result.at[:, pl.ds(row * slab, slab), :],
            dst_ref=out_hbm.at[:, :, pl.ds(pl.multiple_of(row_me * width, width), width)],
            send_sem=send_sems.at[13],
            recv_sem=recv_sems.at[13],
            device_id={"rows": row},
            device_id_type=MESH,
        ).start()
        return carry

    lax.fori_loop(1, n_rows, gather, 0)
    pltpu.make_async_copy(
        result.at[:, pl.ds(row_me * slab, slab), :],
        out_hbm.at[:, :, pl.ds(pl.multiple_of(row_me * width, width), width)],
        recv_sems.at[13],
    ).start()
    pltpu.make_async_copy(out_hbm, out_hbm, recv_sems.at[13]).wait()
    rest = total - slab
    for i in range(3):
        block = sky.at[i, 0:rest, :]
        pltpu.make_async_copy(block, block, send_sems.at[i]).wait()
    for slot in range(10):
        block = sent.at[slot, 0 : (groups - 1) * lines, :]
        pltpu.make_async_copy(block, block, send_sems.at[3 + slot]).wait()
    block = result.at[:, 0:rest, :]
    pltpu.make_async_copy(block, block, send_sems.at[13]).wait()


def body(sizes, constants, sky_maps, band_cuts, filters, wiener, response):
    rows, fields, local, width = sizes
    groups = rows * fields
    total = groups * local

    def grid(value):
        count = value.shape[0]
        value = value.reshape(count, local, width, groups)
        return value.transpose(0, 2, 1, 3).reshape(count, width * local, groups)

    half = width * local
    anywhere = pl.BlockSpec(memory_space=pl.ANY)
    return pl.pallas_call(
        functools.partial(kernel, sizes),
        out_shape=jax.ShapeDtypeStruct((2, *sky_maps.shape[1:]), F32),
        in_specs=[pl.BlockSpec(memory_space=pltpu.SMEM)] + [anywhere] * 8,
        out_specs=anywhere,
        scratch_shapes=[
            pltpu.VMEM((3, total, width), F32),
            pltpu.VMEM((6, half, groups), F32),
            pltpu.VMEM((2, 2 * total, 2 * total), BF16),
            pltpu.VMEM((2, 2 * total, 2 * total), BF16),
            pltpu.VMEM((2, 2 * total, 2 * total), BF16),
            pltpu.VMEM((2, 2 * total, 2 * total), BF16),
            pltpu.VMEM((2, half, 2 * half), BF16),
            pltpu.VMEM((2, half, 2 * half), BF16),
            pltpu.VMEM((2, groups, width), F32),
            pltpu.VMEM((11, groups, half), F32),
            pltpu.VMEM((10, 2 * total, width), F32),
            pltpu.VMEM((10, 2 * total, width), F32),
            pltpu.VMEM((2, total, width), F32),
            pltpu.SemaphoreType.DMA((14,)),
            pltpu.SemaphoreType.DMA((14,)),
            pltpu.SemaphoreType.DMA((7,)),
        ],
        compiler_params=pltpu.CompilerParams(
            collective_id=0, has_side_effects=True, vmem_limit_bytes=40 * 1024 * 1024
        ),
    )(
        band_cuts,
        sky_maps,
        grid(filters),
        grid(wiener),
        grid(response[None]),
        *(jnp.asarray(value) for value in constants),
    )


def solution(mesh):
    placed = (
        P("sims", "rows", "fields"),
        P(),
        P(None, ("rows", "fields"), None),
        P(None, ("rows", "fields"), None),
        P(("rows", "fields"), None),
    )
    rows, fields = mesh.shape["rows"], mesh.shape["fields"]
    groups = rows * fields

    def run(sky_maps, band_cuts, filters, wiener, response):
        sizes = (rows, fields, filters.shape[1] // groups, filters.shape[2] // groups)
        constants = tables(*sizes)
        return jax.shard_map(
            functools.partial(body, sizes, constants),
            mesh=mesh,
            in_specs=placed,
            out_specs=P("sims", "rows", "fields"),
            check_vma=False,
        )(sky_maps, band_cuts, filters, wiener, response)

    return run
```

profile of v0, /device:TPU:513, one launch (start us, length us, event | category | flops | bytes accessed | tf_op | source)
XLA Modules:
  0.0 146.9 jit_solution(13544429140858674091)
XLA Ops:
  0.0 0.0 copy-start.8
  0.0 0.7 copy-done.8
  0.7 0.0 copy-start
  0.7 1.2 copy-done
  1.9 0.0 copy-start.1
  1.9 1.2 copy-done.1
  3.1 0.0 copy-start.2
  3.1 1.0 copy-done.2
  4.1 0.0 copy-start.3
  4.2 1.0 copy-done.3
  5.1 0.0 copy-start.4
  5.1 1.0 copy-done.4
  6.1 0.0 copy-start.5
  6.1 0.9 copy-done.5
  7.1 0.0 copy-start.6
  7.1 0.9 copy-done.6
  8.0 0.0 copy-start.7
  8.0 0.9 copy-done.7
  8.9 137.2 %shard_map.91 = f32[2,16,2048]{2,1,0:T(8,128)S(1)} custom-call(s32[6]{0:T(128)S(1)} %copy-done.8, f32[3,16,2048]{2,1,0:T(8,128)S(1)} %copy-done.3, f32[3,256,128]{2,1,0:T(8,128)S(1)} %bitcast.15, f32[2,256,128]{2,1,0:T(8,128)S(1)} %bitcast.16, f32[1,256,128]{2,1,0:T(8,128)S(1)} %bitcast.17, bf16[2,512,512]{2,1,0:T(8,128)(2,1)S(1)} %copy-done.1, ...), custom_call_target="tpu_custom_call" | custom-call | tf_op jit(solution)/shard_map/pallas_call | solution.py:359
  146.2 0.7 copy.14
Async XLA Ops:
  0.0 0.7 copy-start.8
  0.7 1.2 copy-start
  1.9 1.2 copy-start.1
  3.1 1.0 copy-start.2
  4.1 1.0 copy-start.3
  5.1 1.0 copy-start.4
  6.1 0.9 copy-start.5
  7.1 0.9 copy-start.6
  8.0 0.9 copy-start.7
where the time goes:
time: 147 us
  Pallas kernels  137 us (93%)
  local copies, waits for them, and re-layouts  9.6 us (7%)
    pallas_call x1, Pallas kernels, body(): pl.pallas_call(functools.partial(kernel, sizes), out_shape=jax.ShapeDtype...  137 us
    unnamed x19, local copies, waits for them, and re-layouts  9.6 us

commit v1 on v0

v1 whole, which is shorter than its diff:
```python
import functools
import math

import jax
import jax.numpy as jnp
import numpy as np
from jax import lax
from jax.experimental import pallas as pl
from jax.experimental.pallas import tpu as pltpu
from jax.sharding import PartitionSpec as P

MESH = pl.DeviceIdType.MESH
F32 = jnp.float32
BF16 = jnp.bfloat16


def halves(table):
    high = table.astype(np.float32).astype(BF16)
    low = (table - high.astype(np.float64)).astype(np.float32).astype(BF16)
    return np.stack([np.asarray(high), np.asarray(low)])


def phases(left, right, period):
    angles = 2.0 * math.pi / period * (left[:, None] * right[None, :] % period)
    return np.cos(angles), np.sin(angles)


def tables(rows, fields, local, width):
    groups = rows * fields
    total = groups * local
    length = groups * width
    cos, sin = phases(np.arange(total), np.arange(total), total)
    forward = np.stack([np.concatenate([cos, sin], 1), np.concatenate([-sin, cos], 1)])
    forward = forward.reshape(2, groups, local, 2 * total).transpose(2, 1, 0, 3)
    forward = forward.reshape(2 * total, 2 * total)
    place = np.arange(groups)
    block = place % fields * rows + place // fields
    cos, sin = phases(np.arange(groups), block, groups)
    signed = np.stack([np.stack([cos, sin]), np.stack([-sin, cos])])
    mixed = signed.transpose(0, 2, 3, 1).reshape(2 * groups, 2 * groups)
    within = np.concatenate(phases(np.arange(width), np.arange(width), width), 1)
    cos, sin = phases(np.arange(groups), np.arange(width), length)
    twiddle = np.stack([cos, sin]).astype(np.float32)
    return (
        halves(forward),
        halves(forward.T),
        halves(mixed),
        halves(mixed.T),
        halves(within),
        twiddle,
    )


def dot(left, right):
    return jnp.dot(left, right, preferred_element_type=F32)


def split(value):
    high = value.astype(BF16)
    return high, (value - high.astype(F32)).astype(BF16)


def table_dot(table, value):
    high, low = split(value)
    return dot(table[0], high) + dot(table[0], low) + dot(table[1], high)


def dot_table(value, table):
    high, low = split(value)
    return dot(high, table[0]) + dot(low, table[0]) + dot(high, table[1])


def kernel(
    sizes,
    cuts,
    sky_hbm,
    filters_hbm,
    wiener_hbm,
    response_hbm,
    fwd_rows_hbm,
    inv_rows_hbm,
    fwd_across_hbm,
    inv_across_hbm,
    within_hbm,
    twiddle_hbm,
    out_hbm,
    sky,
    raw,
    fwd_rows,
    inv_rows,
    fwd_across,
    inv_across,
    within,
    twiddle,
    weights,
    sent,
    held,
    result,
    send_sems,
    recv_sems,
    load_sems,
):
    n_rows, n_fields, local, width = sizes
    groups = n_rows * n_fields
    total = groups * local
    length = groups * width
    slab = total // n_rows
    span = 2 * groups
    row_me = lax.axis_index("rows")
    field_me = lax.axis_index("fields")
    me = row_me * n_fields + field_me
    fields = [lax.rem(field_me + i, n_fields) for i in range(n_fields)]

    def everyone(visit):
        for field in fields[1:]:
            visit(row_me, field)

        def turn(step, carry):
            row = lax.rem(row_me + step, n_rows)
            for field in fields:
                visit(row, field)
            return carry

        lax.fori_loop(1, n_rows, turn, 0)

    barrier = pltpu.get_barrier_semaphore()

    def greet(row, field):
        pl.semaphore_signal(
            barrier, inc=1, device_id={"rows": row, "fields": field}, device_id_type=MESH
        )

    everyone(greet)

    loads = [
        pltpu.make_async_copy(source, target, load_sems.at[i])
        for i, (source, target) in enumerate(
            [
                (fwd_rows_hbm, fwd_rows),
                (filters_hbm, raw.at[0:3]),
                (wiener_hbm, raw.at[3:5]),
                (response_hbm, raw.at[5:6]),
                (fwd_across_hbm, fwd_across),
                (within_hbm, within),
                (twiddle_hbm, twiddle),
                (inv_across_hbm, inv_across),
                (inv_rows_hbm, inv_rows),
            ]
        )
    ]
    for load in loads:
        load.start()

    shape = (groups, local * width)
    k = lax.broadcasted_iota(jnp.int32, shape, 0)
    lane = lax.broadcasted_iota(jnp.int32, shape, 1)
    kx = groups * (lane % width) + k
    kx = jnp.where(kx < length // 2, kx, kx - length)
    ky = local * me + lane // width
    ky = jnp.where(ky < total // 2, ky, ky - total)
    sy = (length // total) * ky
    k2 = kx * kx + sy * sy

    def band(i):
        low, high = cuts[2 * i], cuts[2 * i + 1]
        return jnp.where((k2 >= low * low) & (k2 <= high * high), 1.0, 0.0).astype(F32)

    floor = jnp.maximum(k2, 1).astype(F32)
    weights[0] = band(0)
    weights[2] = band(1)
    weights[5] = band(2)
    weights[7] = (kx * kx - sy * sy).astype(F32) / floor
    weights[8] = (2 * kx * sy).astype(F32) / floor
    weights[9] = (2 * kx).astype(F32) / length
    weights[10] = (2 * ky).astype(F32) / total

    pl.semaphore_wait(barrier, groups - 1)

    def columns(row):
        return pl.ds(pl.multiple_of(row * width, width), width)

    for i in range(3):

        def scatter(step, carry, i=i):
            row = lax.rem(row_me + step, n_rows)
            pltpu.make_async_remote_copy(
                src_ref=sky_hbm.at[i, :, columns(row)],
                dst_ref=sky.at[i, pl.ds(row_me * slab, slab), :],
                send_sem=send_sems.at[i],
                recv_sem=recv_sems.at[i],
                device_id={"rows": row},
                device_id_type=MESH,
            ).start()
            return carry

        lax.fori_loop(1, n_rows, scatter, 0)
        pltpu.make_async_copy(
            sky_hbm.at[i, :, columns(row_me)],
            sky.at[i, pl.ds(row_me * slab, slab), :],
            recv_sems.at[i],
        ).start()

    def exchange(slot, part, sem):
        def hand(row, field):
            pltpu.make_async_remote_copy(
                src_ref=sent.at[slot, part, pl.ds((row * n_fields + field) * 2, 2), :],
                dst_ref=held.at[slot, part, pl.ds(me * 2, 2), :],
                send_sem=send_sems.at[sem],
                recv_sem=recv_sems.at[sem],
                device_id={"rows": row, "fields": field},
                device_id_type=MESH,
            ).start()

        everyone(hand)
        pltpu.make_async_copy(
            sent.at[slot, part, pl.ds(me * 2, 2), :],
            held.at[slot, part, pl.ds(me * 2, 2), :],
            recv_sems.at[sem],
        ).start()

    def arrive(slot, part, sem):
        block = held.at[slot, part]
        pltpu.make_async_copy(block, block, recv_sems.at[sem]).wait()

    both = slice(0, local)

    def sides(value, count):
        return jnp.concatenate([value] * count, axis=1)

    def stacked(real, imag):
        count = real.shape[1] // width
        return jnp.concatenate(
            [v[:, i * width : (i + 1) * width] for v in (real, imag) for i in range(count)], axis=0
        )

    def inner(real, imag, sign):
        count = real.shape[1] // width
        out = dot_table(stacked(real, imag), within)
        half = count * groups
        real = out[:half, :width] - sign * out[half:, width:]
        imag = out[half:, :width] + sign * out[:half, width:]
        parts = [
            jnp.concatenate([v[i * groups : (i + 1) * groups] for i in range(count)], axis=1)
            for v in (real, imag)
        ]
        return parts[0], parts[1]

    def columns_forward(slot, rows):
        value = jnp.concatenate([held[slot, i] for i in rows], axis=1)
        mixed = table_dot(fwd_across, value)
        real, imag = mixed[:groups], mixed[groups:]
        cos, sin = sides(twiddle[0], len(rows)), sides(twiddle[1], len(rows))
        return inner(real * cos + imag * sin, imag * cos - real * sin, -1.0)

    def columns_inverse(real, imag):
        count = real.shape[1] // width
        real, imag = inner(real, imag, 1.0)
        cos, sin = sides(twiddle[0], count), sides(twiddle[1], count)
        turned = jnp.concatenate([real * cos - imag * sin, imag * cos + real * sin], axis=0)
        return table_dot(inv_across, turned)

    loads[0].wait()
    for i in range(3):
        pltpu.make_async_copy(sky.at[i], sky.at[i], recv_sems.at[i]).wait()
        high, low = split(sky[i])
        spectra = (
            dot(fwd_rows[0, :, :total], high)
            + dot(fwd_rows[0, :, :total], low)
            + dot(fwd_rows[1, :, :total], high)
        )
        for j in range(local):
            sent[i, j] = spectra[j * span : (j + 1) * span]
        exchange(i, both, 3 + i)

    for load in loads[1:]:
        load.wait()

    def grid(i):
        rows = [raw[i, pl.ds(j, width, stride=local), :].T for j in range(local)]
        return jnp.concatenate(rows, axis=1)

    norm = 1.0 / (length * total)
    weights[0] = weights[0] * grid(0) * norm
    weights[1] = grid(3)
    band_pol = weights[2] * norm
    weights[2] = band_pol * grid(1)
    weights[3] = band_pol * grid(2)
    weights[4] = grid(4)
    out_weight = weights[5] * grid(5) * norm
    weights[5] = out_weight * weights[10]
    weights[6] = out_weight * weights[9]

    def leg(slot, real, imag):
        out = columns_inverse(real, imag)
        for j in range(local):
            sent[slot, j] = out[:, j * width : (j + 1) * width]
        exchange(slot, both, 3 + slot)

    all_rows = list(range(local))
    arrive(0, both, 3)
    t_real, t_imag = columns_forward(0, all_rows)
    t_real, t_imag = weights[0] * t_real, weights[0] * t_imag
    leg(3, t_real, t_imag)
    w_real, w_imag = weights[1] * t_real, weights[1] * t_imag
    ux, uy = weights[9], weights[10]
    leg(4, -uy * w_real - ux * w_imag, ux * w_real - uy * w_imag)
    arrive(1, both, 4)
    q_real, q_imag = columns_forward(1, all_rows)
    arrive(2, both, 5)
    u_real, u_imag = columns_forward(2, all_rows)
    cos_two, sin_two = weights[7], weights[8]
    e_real = -weights[2] * (cos_two * q_real + sin_two * u_real)
    e_imag = -weights[2] * (cos_two * q_imag + sin_two * u_imag)
    b_real = weights[3] * (sin_two * q_real - cos_two * u_real)
    b_imag = weights[3] * (sin_two * q_imag - cos_two * u_imag)
    s_real, s_imag = e_real - b_imag, e_imag + b_real
    leg(5, sin_two * s_imag - cos_two * s_real, -cos_two * s_imag - sin_two * s_real)
    w_real, w_imag = weights[4] * e_real, weights[4] * e_imag
    w_real, w_imag = sin_two * w_imag - cos_two * w_real, -cos_two * w_imag - sin_two * w_real
    leg(6, -uy * w_real - ux * w_imag, ux * w_real - uy * w_imag)
    leg(7, uy * w_real - ux * w_imag, ux * w_real + uy * w_imag)

    def to_maps(slot):
        arrive(slot, both, 3 + slot)
        value = jnp.concatenate([held[slot, j] for j in range(local)], axis=0)
        maps = table_dot(inv_rows, value)
        return maps[:total], maps[total:]

    a_real, a_imag = to_maps(3)
    g_real, g_imag = to_maps(4)
    c_real = a_real * g_real - a_imag * g_imag
    c_imag = a_real * g_imag + a_imag * g_real
    p_real, p_imag = to_maps(5)
    h_real, h_imag = to_maps(6)
    c_real = c_real + 0.5 * (p_real * h_real + p_imag * h_imag)
    c_imag = c_imag + 0.5 * (p_real * h_imag - p_imag * h_real)
    h_real, h_imag = to_maps(7)
    c_real = c_real + 0.5 * (p_real * h_real + p_imag * h_imag)
    c_imag = c_imag + 0.5 * (p_imag * h_real - p_real * h_imag)
    current = jnp.concatenate([c_real, c_imag], axis=0)
    high, low = split(current)
    for j in range(local):
        part = slice(j * span, (j + 1) * span)
        sent[8, j] = (
            dot(fwd_rows[0, part], high)
            + dot(fwd_rows[0, part], low)
            + dot(fwd_rows[1, part], high)
        )
        exchange(8, j, 11 + j)
    for j in range(local):
        arrive(8, j, 11 + j)
        c_real, c_imag = columns_forward(8, [j])
        lanes = slice(j * width, (j + 1) * width)
        down, along = weights[5, :, lanes], weights[6, :, lanes]
        sent[9, j] = columns_inverse(down * c_real - along * c_imag, along * c_real + down * c_imag)
        exchange(9, j, 11 + local + j)
    maps = None
    for j in range(local):
        arrive(9, j, 11 + local + j)
        part = slice(j * span, (j + 1) * span)
        high, low = split(held[9, j])
        added = (
            dot(inv_rows[0, :, part], high)
            + dot(inv_rows[0, :, part], low)
            + dot(inv_rows[1, :, part], high)
        )
        maps = added if maps is None else maps + added
    last = 11 + 2 * local
    result[0] = maps[:total]
    result[1] = maps[total:]

    def gather(step, carry):
        row = lax.rem(row_me + step, n_rows)
        pltpu.make_async_remote_copy(
            src_ref=result.at[:, pl.ds(row * slab, slab), :],
            dst_ref=out_hbm.at[:, :, columns(row_me)],
            send_sem=send_sems.at[last],
            recv_sem=recv_sems.at[last],
            device_id={"rows": row},
            device_id_type=MESH,
        ).start()
        return carry

    lax.fori_loop(1, n_rows, gather, 0)
    pltpu.make_async_copy(
        result.at[:, pl.ds(row_me * slab, slab), :],
        out_hbm.at[:, :, columns(row_me)],
        recv_sems.at[last],
    ).start()
    pltpu.make_async_copy(out_hbm, out_hbm, recv_sems.at[last]).wait()
    rest = total - slab

    def gone(block, sem):
        pltpu.make_async_copy(block, block, send_sems.at[sem]).wait()

    for i in range(3):
        gone(sky.at[i, 0:rest, :], i)
    for slot in range(8):
        gone(sent.at[slot, both, 0 : span - 2, :], 3 + slot)
    for j in range(local):
        gone(sent.at[8, j, 0 : span - 2, :], 11 + j)
        gone(sent.at[9, j, 0 : span - 2, :], 11 + local + j)
    gone(result.at[:, 0:rest, :], last)


def body(sizes, constants, sky_maps, band_cuts, filters, wiener, response):
    rows, fields, local, width = sizes
    groups = rows * fields
    total = groups * local

    def grid(value):
        count = value.shape[0]
        value = value.reshape(count, local, width, groups)
        return value.transpose(0, 2, 1, 3).reshape(count, width * local, groups)

    anywhere = pl.BlockSpec(memory_space=pl.ANY)
    count = 12 + 2 * local
    return pl.pallas_call(
        functools.partial(kernel, sizes),
        out_shape=jax.ShapeDtypeStruct((2, *sky_maps.shape[1:]), F32),
        in_specs=[pl.BlockSpec(memory_space=pltpu.SMEM)] + [anywhere] * 10,
        out_specs=anywhere,
        scratch_shapes=[
            pltpu.VMEM((3, total, width), F32),
            pltpu.VMEM((6, local * width, groups), F32),
            pltpu.VMEM((2, 2 * total, 2 * total), BF16),
            pltpu.VMEM((2, 2 * total, 2 * total), BF16),
            pltpu.VMEM((2, 2 * groups, 2 * groups), BF16),
            pltpu.VMEM((2, 2 * groups, 2 * groups), BF16),
            pltpu.VMEM((2, width, 2 * width), BF16),
            pltpu.VMEM((2, groups, width), F32),
            pltpu.VMEM((11, groups, local * width), F32),
            pltpu.VMEM((10, local, 2 * groups, width), F32),
            pltpu.VMEM((10, local, 2 * groups, width), F32),
            pltpu.VMEM((2, total, width), F32),
            pltpu.SemaphoreType.DMA((count,)),
            pltpu.SemaphoreType.DMA((count,)),
            pltpu.SemaphoreType.DMA((9,)),
        ],
        compiler_params=pltpu.CompilerParams(
            collective_id=0, has_side_effects=True, vmem_limit_bytes=60 * 1024 * 1024
        ),
    )(
        band_cuts,
        sky_maps,
        grid(filters),
        grid(wiener),
        grid(response[None]),
        *(jnp.asarray(value) for value in constants),
    )


def solution(mesh):
    placed = (
        P("sims", "rows", "fields"),
        P(),
        P(None, ("rows", "fields"), None),
        P(None, ("rows", "fields"), None),
        P(("rows", "fields"), None),
    )
    rows, fields = mesh.shape["rows"], mesh.shape["fields"]
    groups = rows * fields

    def run(sky_maps, band_cuts, filters, wiener, response):
        sizes = (rows, fields, filters.shape[1] // groups, filters.shape[2] // groups)
        constants = tables(*sizes)
        return jax.shard_map(
            functools.partial(body, sizes, constants),
            mesh=mesh,
            in_specs=placed,
            out_specs=P("sims", "rows", "fields"),
            check_vma=False,
        )(sky_maps, band_cuts, filters, wiener, response)

    return run
```

time: 147 us -> 128 us (0.87)
  Pallas kernels: 137 us -> 126 us
  local copies, waits for them, and re-layouts: 9.6 us -> 1.67 us
    pallas_call x1, Pallas kernels: 137 us -> 126 us  [body(): pl.pallas_call(functools.partial(kernel, sizes), out_shape=jax.ShapeDtype...]
    unnamed x19 -> x1, local copies, waits for them, and re-layouts: 9.6 us -> 1.67 us
where the time goes in v1:
time: 128 us
  Pallas kernels  126 us (98%)
  local copies, waits for them, and re-layouts  1.67 us (1%)
    pallas_call x1, Pallas kernels, body(): pl.pallas_call(functools.partial(kernel, sizes), out_shape=jax.ShapeDtype...  126 us

profile of v1, /device:TPU:513, one launch (start us, length us, event | category | flops | bytes accessed | tf_op | source)
XLA Modules:
  0.0 128.1 jit_solution(18388902795740254263)
XLA Ops:
  0.0 126.4 %shard_map.109 = f32[2,16,2048]{2,1,0:T(8,128)} custom-call(s32[6]{0:T(128)} %cuts.1, f32[3,16,2048]{2,1,0:T(8,128)} %sky_hbm.1, f32[3,256,128]{2,1,0:T(8,128)} %bitcast.15, f32[2,256,128]{2,1,0:T(8,128)} %bitcast.16, f32[1,256,128]{2,1,0:T(8,128)} %bitcast.17, bf16[2,512,512]{2,1,0:T(8,128)(2,1)} %constant.12.clone.fwd_rows_hbm, ...), custom_call_target="tpu_custom_call" | custom-call | tf_op jit(solution)/shard_map/pallas_call | solution.py:418
  126.4 1.7 %copy.16 = f32[2,16,2048]{2,1,0:T(8,128)} copy(f32[2,16,2048]{2,1,0:T(8,128)} %shard_map.109) | data formatting | bytes 524288

commit v2 on v1

--- a/solution.py
+++ b/solution.py
@@ -72,7 +72,7 @@
 
 def kernel(
     sizes,
-    cuts,
+    cuts_hbm,
     sky_hbm,
     filters_hbm,
     wiener_hbm,
@@ -83,7 +83,9 @@
     inv_across_hbm,
     within_hbm,
     twiddle_hbm,
-    out_hbm,
+    out,
+    cuts,
+    local_sky,
     sky,
     raw,
     fwd_rows,
@@ -111,17 +113,20 @@
     me = row_me * n_fields + field_me
     fields = [lax.rem(field_me + i, n_fields) for i in range(n_fields)]
 
+    def far_row(step):
+        side = 1 - 2 * (step % 2)
+        return lax.rem(row_me + n_rows // 2 + side * ((step + 1) // 2), n_rows)
+
     def everyone(visit):
-        for field in fields[1:]:
-            visit(row_me, field)
-
         def turn(step, carry):
-            row = lax.rem(row_me + step, n_rows)
+            row = far_row(step)
             for field in fields:
                 visit(row, field)
             return carry
 
-        lax.fori_loop(1, n_rows, turn, 0)
+        lax.fori_loop(0, n_rows - 1, turn, 0)
+        for field in fields[1:]:
+            visit(row_me, field)
 
     barrier = pltpu.get_barrier_semaphore()
 
@@ -136,6 +141,8 @@
         pltpu.make_async_copy(source, target, load_sems.at[i])
         for i, (source, target) in enumerate(
             [
+                (cuts_hbm, cuts),
+                (sky_hbm, local_sky),
                 (fwd_rows_hbm, fwd_rows),
                 (filters_hbm, raw.at[0:3]),
                 (wiener_hbm, raw.at[3:5]),
@@ -151,6 +158,7 @@
     for load in loads:
         load.start()
 
+    loads[0].wait()
     shape = (groups, local * width)
     k = lax.broadcasted_iota(jnp.int32, shape, 0)
     lane = lax.broadcasted_iota(jnp.int32, shape, 1)
@@ -174,6 +182,7 @@
     weights[9] = (2 * kx).astype(F32) / length
     weights[10] = (2 * ky).astype(F32) / total
 
+    loads[1].wait()
     pl.semaphore_wait(barrier, groups - 1)
 
     def columns(row):
@@ -182,9 +191,9 @@
     for i in range(3):
 
         def scatter(step, carry, i=i):
-            row = lax.rem(row_me + step, n_rows)
+            row = far_row(step)
             pltpu.make_async_remote_copy(
-                src_ref=sky_hbm.at[i, :, columns(row)],
+                src_ref=local_sky.at[i, :, columns(row)],
                 dst_ref=sky.at[i, pl.ds(row_me * slab, slab), :],
                 send_sem=send_sems.at[i],
                 recv_sem=recv_sems.at[i],
@@ -193,9 +202,9 @@
             ).start()
             return carry
 
-        lax.fori_loop(1, n_rows, scatter, 0)
+        lax.fori_loop(0, n_rows - 1, scatter, 0)
         pltpu.make_async_copy(
-            sky_hbm.at[i, :, columns(row_me)],
+            local_sky.at[i, :, columns(row_me)],
             sky.at[i, pl.ds(row_me * slab, slab), :],
             recv_sems.at[i],
         ).start()
@@ -259,7 +268,7 @@
         turned = jnp.concatenate([real * cos - imag * sin, imag * cos + real * sin], axis=0)
         return table_dot(inv_across, turned)
 
-    loads[0].wait()
+    loads[2].wait()
     for i in range(3):
         pltpu.make_async_copy(sky.at[i], sky.at[i], recv_sems.at[i]).wait()
         high, low = split(sky[i])
@@ -272,7 +281,7 @@
             sent[i, j] = spectra[j * span : (j + 1) * span]
         exchange(i, both, 3 + i)
 
-    for load in loads[1:]:
+    for load in loads[3:]:
         load.wait()
 
     def grid(i):
@@ -370,10 +379,10 @@
     result[1] = maps[total:]
 
     def gather(step, carry):
-        row = lax.rem(row_me + step, n_rows)
+        row = far_row(step)
         pltpu.make_async_remote_copy(
             src_ref=result.at[:, pl.ds(row * slab, slab), :],
-            dst_ref=out_hbm.at[:, :, columns(row_me)],
+            dst_ref=out.at[:, :, columns(row_me)],
             send_sem=send_sems.at[last],
             recv_sem=recv_sems.at[last],
             device_id={"rows": row},
@@ -381,13 +390,13 @@
         ).start()
         return carry
 
-    lax.fori_loop(1, n_rows, gather, 0)
+    lax.fori_loop(0, n_rows - 1, gather, 0)
     pltpu.make_async_copy(
         result.at[:, pl.ds(row_me * slab, slab), :],
-        out_hbm.at[:, :, columns(row_me)],
+        out.at[:, :, columns(row_me)],
         recv_sems.at[last],
     ).start()
-    pltpu.make_async_copy(out_hbm, out_hbm, recv_sems.at[last]).wait()
+    pltpu.make_async_copy(out, out, recv_sems.at[last]).wait()
     rest = total - slab
 
     def gone(block, sem):
@@ -417,10 +426,12 @@
     count = 12 + 2 * local
     return pl.pallas_call(
         functools.partial(kernel, sizes),
-        out_shape=jax.ShapeDtypeStruct((2, *sky_maps.shape[1:]), F32),
-        in_specs=[pl.BlockSpec(memory_space=pltpu.SMEM)] + [anywhere] * 10,
-        out_specs=anywhere,
+        out_shape=pltpu.VMEM((2, *sky_maps.shape[1:]), F32),
+        in_specs=[anywhere] * 11,
+        out_specs=pl.BlockSpec(memory_space=pltpu.VMEM),
         scratch_shapes=[
+            pltpu.SMEM(band_cuts.shape, jnp.int32),
+            pltpu.VMEM(sky_maps.shape, F32),
             pltpu.VMEM((3, total, width), F32),
             pltpu.VMEM((6, local * width, groups), F32),
             pltpu.VMEM((2, 2 * total, 2 * total), BF16),
@@ -435,7 +446,7 @@
             pltpu.VMEM((2, total, width), F32),
             pltpu.SemaphoreType.DMA((count,)),
             pltpu.SemaphoreType.DMA((count,)),
-            pltpu.SemaphoreType.DMA((9,)),
+            pltpu.SemaphoreType.DMA((11,)),
         ],
         compiler_params=pltpu.CompilerParams(
             collective_id=0, has_side_effects=True, vmem_limit_bytes=60 * 1024 * 1024

time: 128 us -> 118 us (0.922)
  Pallas kernels: 126 us -> 118 us
    pallas_call x1, Pallas kernels: 126 us -> 118 us  [body(): pl.pallas_call(functools.partial(kernel, sizes), out_shape=pltpu.VMEM((2,...]
where the time goes in v2:
time: 118 us
  Pallas kernels  118 us (100%)
    pallas_call x1, Pallas kernels, body(): pl.pallas_call(functools.partial(kernel, sizes), out_shape=pltpu.VMEM((2,...  118 us

profile of v2, /device:TPU:513, one launch (start us, length us, event | category | flops | bytes accessed | tf_op | source)
XLA Modules:
  0.0 118.3 jit_solution(885703034912166871)
XLA Ops:
  0.0 117.5 %shard_map.109 = f32[2,16,2048]{2,1,0:T(8,128)S(1)} custom-call(s32[6]{0:T(128)} %cuts_hbm.1, f32[3,16,2048]{2,1,0:T(8,128)} %sky_hbm.1, f32[3,256,128]{2,1,0:T(8,128)} %bitcast.15, f32[2,256,128]{2,1,0:T(8,128)} %bitcast.16, f32[1,256,128]{2,1,0:T(8,128)} %bitcast.17, bf16[2,512,512]{2,1,0:T(8,128)(2,1)} %constant.12.clone.fwd_rows_hbm, ...), custom_call_target="tpu_custom_call" | custom-call | tf_op jit(solution)/shard_map/pallas_call | solution.py:427
  117.6 0.7 copy.16

commit v3 on v2

--- a/solution.py
+++ b/solution.py
@@ -98,6 +98,7 @@
     sent,
     held,
     result,
+    stage,
     send_sems,
     recv_sems,
     load_sems,
@@ -254,12 +255,33 @@
         ]
         return parts[0], parts[1]
 
-    def columns_forward(slot, rows):
-        value = jnp.concatenate([held[slot, i] for i in rows], axis=1)
-        mixed = table_dot(fwd_across, value)
+    def columns_forward(mixed):
         real, imag = mixed[:groups], mixed[groups:]
-        cos, sin = sides(twiddle[0], len(rows)), sides(twiddle[1], len(rows))
+        cos, sin = sides(twiddle[0], local), sides(twiddle[1], local)
         return inner(real * cos + imag * sin, imag * cos - real * sin, -1.0)
+
+    def field_forward(slot):
+        value = jnp.concatenate([held[slot, j] for j in range(local)], axis=1)
+        return columns_forward(table_dot(fwd_across, value))
+
+    share = width // local
+
+    def to_parts(value):
+        return [
+            jnp.concatenate(
+                [
+                    value[:, j * width + h * share : j * width + (h + 1) * share]
+                    for j in range(local)
+                ],
+                axis=1,
+            )
+            for h in range(local)
+        ]
+
+    def from_parts(parts):
+        return jnp.concatenate(
+            [part[:, j * share : (j + 1) * share] for j in range(local) for part in parts], axis=1
+        )
 
     def columns_inverse(real, imag):
         count = real.shape[1] // width
@@ -299,24 +321,32 @@
     weights[5] = out_weight * weights[10]
     weights[6] = out_weight * weights[9]
 
+    def sem_of(slot, h):
+        return 3 + 3 + (slot - 3) * local + h
+
     def leg(slot, real, imag):
-        out = columns_inverse(real, imag)
-        for j in range(local):
-            sent[slot, j] = out[:, j * width : (j + 1) * width]
-        exchange(slot, both, 3 + slot)
-
-    all_rows = list(range(local))
+        parts = to_parts(columns_inverse(real, imag))
+        for h in range(local):
+            sent[slot, h] = parts[h]
+
+    def send(slots):
+        for h in range(local):
+            for slot in slots:
+                exchange(slot, h, sem_of(slot, h))
+
     arrive(0, both, 3)
-    t_real, t_imag = columns_forward(0, all_rows)
+    t_real, t_imag = field_forward(0)
     t_real, t_imag = weights[0] * t_real, weights[0] * t_imag
     leg(3, t_real, t_imag)
+    send([3])
     w_real, w_imag = weights[1] * t_real, weights[1] * t_imag
     ux, uy = weights[9], weights[10]
     leg(4, -uy * w_real - ux * w_imag, ux * w_real - uy * w_imag)
+    send([4])
     arrive(1, both, 4)
-    q_real, q_imag = columns_forward(1, all_rows)
+    q_real, q_imag = field_forward(1)
     arrive(2, both, 5)
-    u_real, u_imag = columns_forward(2, all_rows)
+    u_real, u_imag = field_forward(2)
     cos_two, sin_two = weights[7], weights[8]
     e_real = -weights[2] * (cos_two * q_real + sin_two * u_real)
     e_imag = -weights[2] * (cos_two * q_imag + sin_two * u_imag)
@@ -326,77 +356,74 @@
     leg(5, sin_two * s_imag - cos_two * s_real, -cos_two * s_imag - sin_two * s_real)
     w_real, w_imag = weights[4] * e_real, weights[4] * e_imag
     w_real, w_imag = sin_two * w_imag - cos_two * w_real, -cos_two * w_imag - sin_two * w_real
-    leg(6, -uy * w_real - ux * w_imag, ux * w_real - uy * w_imag)
-    leg(7, uy * w_real - ux * w_imag, ux * w_real + uy * w_imag)
-
-    def to_maps(slot):
-        arrive(slot, both, 3 + slot)
-        value = jnp.concatenate([held[slot, j] for j in range(local)], axis=0)
+    leg(6, -ux * w_imag, ux * w_real)
+    leg(7, uy * w_real, uy * w_imag)
+    send([5, 6, 7])
+
+    def to_maps(slot, h):
+        arrive(slot, h, sem_of(slot, h))
+        part = held[slot, h]
+        value = jnp.concatenate([part[:, j * share : (j + 1) * share] for j in range(local)], axis=0)
         maps = table_dot(inv_rows, value)
         return maps[:total], maps[total:]
 
-    a_real, a_imag = to_maps(3)
-    g_real, g_imag = to_maps(4)
-    c_real = a_real * g_real - a_imag * g_imag
-    c_imag = a_real * g_imag + a_imag * g_real
-    p_real, p_imag = to_maps(5)
-    h_real, h_imag = to_maps(6)
-    c_real = c_real + 0.5 * (p_real * h_real + p_imag * h_imag)
-    c_imag = c_imag + 0.5 * (p_real * h_imag - p_imag * h_real)
-    h_real, h_imag = to_maps(7)
-    c_real = c_real + 0.5 * (p_real * h_real + p_imag * h_imag)
-    c_imag = c_imag + 0.5 * (p_imag * h_real - p_real * h_imag)
-    current = jnp.concatenate([c_real, c_imag], axis=0)
-    high, low = split(current)
-    for j in range(local):
-        part = slice(j * span, (j + 1) * span)
-        sent[8, j] = (
-            dot(fwd_rows[0, part], high)
-            + dot(fwd_rows[0, part], low)
-            + dot(fwd_rows[1, part], high)
+    products = []
+    for h in range(local):
+        a_real, a_imag = to_maps(3, h)
+        g_real, g_imag = to_maps(4, h)
+        products.append((a_real * g_real - a_imag * g_imag, a_real * g_imag + a_imag * g_real))
+    for h in range(local):
+        c_real, c_imag = products[h]
+        p_real, p_imag = to_maps(5, h)
+        x_real, x_imag = to_maps(6, h)
+        c_real = c_real + (p_real * x_real + p_imag * x_imag)
+        y_real, y_imag = to_maps(7, h)
+        c_imag = c_imag - (p_real * y_imag - p_imag * y_real)
+        spectra = table_dot(fwd_rows, jnp.concatenate([c_real, c_imag], axis=0))
+        sent[8, h] = jnp.concatenate(
+            [spectra[j * span : (j + 1) * span] for j in range(local)], axis=1
         )
-        exchange(8, j, 11 + j)
-    for j in range(local):
-        arrive(8, j, 11 + j)
-        c_real, c_imag = columns_forward(8, [j])
-        lanes = slice(j * width, (j + 1) * width)
-        down, along = weights[5, :, lanes], weights[6, :, lanes]
-        sent[9, j] = columns_inverse(down * c_real - along * c_imag, along * c_real + down * c_imag)
-        exchange(9, j, 11 + local + j)
-    maps = None
-    for j in range(local):
-        arrive(9, j, 11 + local + j)
-        part = slice(j * span, (j + 1) * span)
-        high, low = split(held[9, j])
-        added = (
-            dot(inv_rows[0, :, part], high)
-            + dot(inv_rows[0, :, part], low)
-            + dot(inv_rows[1, :, part], high)
-        )
-        maps = added if maps is None else maps + added
-    last = 11 + 2 * local
-    result[0] = maps[:total]
-    result[1] = maps[total:]
-
-    def gather(step, carry):
-        row = far_row(step)
-        pltpu.make_async_remote_copy(
-            src_ref=result.at[:, pl.ds(row * slab, slab), :],
-            dst_ref=out.at[:, :, columns(row_me)],
-            send_sem=send_sems.at[last],
-            recv_sem=recv_sems.at[last],
-            device_id={"rows": row},
-            device_id_type=MESH,
+        exchange(8, h, sem_of(8, h))
+    mixed = []
+    for h in range(local):
+        arrive(8, h, sem_of(8, h))
+        mixed.append(table_dot(fwd_across, held[8, h]))
+    c_real, c_imag = columns_forward(from_parts(mixed))
+    down, along = weights[5], weights[6]
+    leg(9, down * c_real - along * c_imag, along * c_real + down * c_imag)
+    send([9])
+    last = 6 + 7 * local
+    for h in range(local):
+        e_real, e_imag = to_maps(9, h)
+        result[h, :, :share] = e_real
+        result[h, :, share : 2 * share] = e_imag
+
+        def gather(step, carry, h=h):
+            row = far_row(step)
+            pltpu.make_async_remote_copy(
+                src_ref=result.at[h, pl.ds(row * slab, slab), :],
+                dst_ref=stage.at[h, pl.ds(row_me * slab, slab), :],
+                send_sem=send_sems.at[last + h],
+                recv_sem=recv_sems.at[last + h],
+                device_id={"rows": row},
+                device_id_type=MESH,
+            ).start()
+            return carry
+
+        lax.fori_loop(0, n_rows - 1, gather, 0)
+        pltpu.make_async_copy(
+            result.at[h, pl.ds(row_me * slab, slab), :],
+            stage.at[h, pl.ds(row_me * slab, slab), :],
+            recv_sems.at[last + h],
         ).start()
-        return carry
-
-    lax.fori_loop(0, n_rows - 1, gather, 0)
-    pltpu.make_async_copy(
-        result.at[:, pl.ds(row_me * slab, slab), :],
-        out.at[:, :, columns(row_me)],
-        recv_sems.at[last],
-    ).start()
-    pltpu.make_async_copy(out, out, recv_sems.at[last]).wait()
+    for h in range(local):
+        pltpu.make_async_copy(stage.at[h], stage.at[h], recv_sems.at[last + h]).wait()
+    for row in range(n_rows):
+        blocks = [stage[h, row * slab : (row + 1) * slab] for h in range(local)]
+        for c in range(2):
+            out[c, :, row * width : (row + 1) * width] = jnp.concatenate(
+                [block[:, c * share : (c + 1) * share] for block in blocks], axis=1
+            )
     rest = total - slab
 
     def gone(block, sem):
@@ -404,12 +431,13 @@
 
     for i in range(3):
         gone(sky.at[i, 0:rest, :], i)
-    for slot in range(8):
-        gone(sent.at[slot, both, 0 : span - 2, :], 3 + slot)
-    for j in range(local):
-        gone(sent.at[8, j, 0 : span - 2, :], 11 + j)
-        gone(sent.at[9, j, 0 : span - 2, :], 11 + local + j)
-    gone(result.at[:, 0:rest, :], last)
+    for i in range(3):
+        gone(sent.at[i, both, 0 : span - 2, :], 3 + i)
+    for slot in range(3, 10):
+        for h in range(local):
+            gone(sent.at[slot, h, 0 : span - 2, :], sem_of(slot, h))
+    for h in range(local):
+        gone(result.at[h, 0:rest, :], last + h)
 
 
 def body(sizes, constants, sky_maps, band_cuts, filters, wiener, response):
@@ -423,7 +451,8 @@
         return value.transpose(0, 2, 1, 3).reshape(count, width * local, groups)
 
     anywhere = pl.BlockSpec(memory_space=pl.ANY)
-    count = 12 + 2 * local
+    count = 6 + 8 * local
+    lanes = 2 * (width // local)
     return pl.pallas_call(
         functools.partial(kernel, sizes),
         out_shape=pltpu.VMEM((2, *sky_maps.shape[1:]), F32),
@@ -443,7 +472,8 @@
             pltpu.VMEM((11, groups, local * width), F32),
             pltpu.VMEM((10, local, 2 * groups, width), F32),
             pltpu.VMEM((10, local, 2 * groups, width), F32),
-            pltpu.VMEM((2, total, width), F32),
+            pltpu.VMEM((local, total, lanes), F32),
+            pltpu.VMEM((local, total, lanes), F32),
             pltpu.SemaphoreType.DMA((count,)),
             pltpu.SemaphoreType.DMA((count,)),
             pltpu.SemaphoreType.DMA((11,)),

time: 118 us -> 125 us (1.059)
  Pallas kernels: 118 us -> 124 us
    pallas_call x1, Pallas kernels: 118 us -> 124 us  [body(): pl.pallas_call(functools.partial(kernel, sizes), out_shape=pltpu.VMEM((2,...]
where the time goes in v3:
time: 125 us
  Pallas kernels  124 us (99%)
    pallas_call x1, Pallas kernels, body(): pl.pallas_call(functools.partial(kernel, sizes), out_shape=pltpu.VMEM((2,...  124 us

profile of v3, /device:TPU:513, one launch (start us, length us, event | category | flops | bytes accessed | tf_op | source)
XLA Modules:
  0.0 124.8 jit_solution(18155473379586598830)
XLA Ops:
  0.0 124.1 %shard_map.109 = f32[2,16,2048]{2,1,0:T(8,128)S(1)} custom-call(s32[6]{0:T(128)} %cuts_hbm.1, f32[3,16,2048]{2,1,0:T(8,128)} %sky_hbm.1, f32[3,256,128]{2,1,0:T(8,128)} %bitcast.15, f32[2,256,128]{2,1,0:T(8,128)} %bitcast.16, f32[1,256,128]{2,1,0:T(8,128)} %bitcast.17, bf16[2,512,512]{2,1,0:T(8,128)(2,1)} %constant.12.clone.fwd_rows_hbm, ...), custom_call_target="tpu_custom_call" | custom-call | tf_op jit(solution)/shard_map/pallas_call | solution.py:456
  124.1 0.7 copy.16

commit v4 on v3

--- a/solution.py
+++ b/solution.py
@@ -120,12 +120,13 @@
 
     def everyone(visit):
         def turn(step, carry):
-            row = far_row(step)
+            offset, side = carry
+            row = lax.rem(row_me + offset, n_rows)
             for field in fields:
                 visit(row, field)
-            return carry
-
-        lax.fori_loop(0, n_rows - 1, turn, 0)
+            return n_rows - 1 + side - offset, 1 - side
+
+        lax.fori_loop(0, n_rows - 1, turn, (jnp.int32(n_rows // 2), jnp.int32(0)))
         for field in fields[1:]:
             visit(row_me, field)
 
@@ -321,28 +322,27 @@
     weights[5] = out_weight * weights[10]
     weights[6] = out_weight * weights[9]
 
+    pair = slice(5, 7)
+
     def sem_of(slot, h):
-        return 3 + 3 + (slot - 3) * local + h
+        if slot < 8:
+            return 8 + 2 * h + slot // 7
+        return 8 + (slot - 6) * local + h
 
     def leg(slot, real, imag):
         parts = to_parts(columns_inverse(real, imag))
         for h in range(local):
             sent[slot, h] = parts[h]
 
-    def send(slots):
-        for h in range(local):
-            for slot in slots:
-                exchange(slot, h, sem_of(slot, h))
-
     arrive(0, both, 3)
     t_real, t_imag = field_forward(0)
     t_real, t_imag = weights[0] * t_real, weights[0] * t_imag
     leg(3, t_real, t_imag)
-    send([3])
+    exchange(3, both, 6)
     w_real, w_imag = weights[1] * t_real, weights[1] * t_imag
     ux, uy = weights[9], weights[10]
     leg(4, -uy * w_real - ux * w_imag, ux * w_real - uy * w_imag)
-    send([4])
+    exchange(4, both, 7)
     arrive(1, both, 4)
     q_real, q_imag = field_forward(1)
     arrive(2, both, 5)
@@ -358,15 +358,18 @@
     w_real, w_imag = sin_two * w_imag - cos_two * w_real, -cos_two * w_imag - sin_two * w_real
     leg(6, -ux * w_imag, ux * w_real)
     leg(7, uy * w_real, uy * w_imag)
-    send([5, 6, 7])
+    for h in range(local):
+        exchange(pair, h, sem_of(5, h))
+        exchange(7, h, sem_of(7, h))
 
     def to_maps(slot, h):
-        arrive(slot, h, sem_of(slot, h))
         part = held[slot, h]
         value = jnp.concatenate([part[:, j * share : (j + 1) * share] for j in range(local)], axis=0)
         maps = table_dot(inv_rows, value)
         return maps[:total], maps[total:]
 
+    arrive(3, both, 6)
+    arrive(4, both, 7)
     products = []
     for h in range(local):
         a_real, a_imag = to_maps(3, h)
@@ -374,9 +377,11 @@
         products.append((a_real * g_real - a_imag * g_imag, a_real * g_imag + a_imag * g_real))
     for h in range(local):
         c_real, c_imag = products[h]
+        arrive(pair, h, sem_of(5, h))
         p_real, p_imag = to_maps(5, h)
         x_real, x_imag = to_maps(6, h)
         c_real = c_real + (p_real * x_real + p_imag * x_imag)
+        arrive(7, h, sem_of(7, h))
         y_real, y_imag = to_maps(7, h)
         c_imag = c_imag - (p_real * y_imag - p_imag * y_real)
         spectra = table_dot(fwd_rows, jnp.concatenate([c_real, c_imag], axis=0))
@@ -391,9 +396,11 @@
     c_real, c_imag = columns_forward(from_parts(mixed))
     down, along = weights[5], weights[6]
     leg(9, down * c_real - along * c_imag, along * c_real + down * c_imag)
-    send([9])
-    last = 6 + 7 * local
-    for h in range(local):
+    for h in range(local):
+        exchange(9, h, sem_of(9, h))
+    last = 8 + 4 * local
+    for h in range(local):
+        arrive(9, h, sem_of(9, h))
         e_real, e_imag = to_maps(9, h)
         result[h, :, :share] = e_real
         result[h, :, share : 2 * share] = e_imag
@@ -431,10 +438,11 @@
 
     for i in range(3):
         gone(sky.at[i, 0:rest, :], i)
-    for i in range(3):
+    for i in range(5):
         gone(sent.at[i, both, 0 : span - 2, :], 3 + i)
-    for slot in range(3, 10):
-        for h in range(local):
+    for h in range(local):
+        gone(sent.at[pair, h, 0 : span - 2, :], sem_of(5, h))
+        for slot in range(7, 10):
             gone(sent.at[slot, h, 0 : span - 2, :], sem_of(slot, h))
     for h in range(local):
         gone(result.at[h, 0:rest, :], last + h)
@@ -451,7 +459,7 @@
         return value.transpose(0, 2, 1, 3).reshape(count, width * local, groups)
 
     anywhere = pl.BlockSpec(memory_space=pl.ANY)
-    count = 6 + 8 * local
+    count = 8 + 5 * local
     lanes = 2 * (width // local)
     return pl.pallas_call(
         functools.partial(kernel, sizes),

time: 125 us -> 117 us (0.936)
  Pallas kernels: 124 us -> 116 us
    pallas_call x1, Pallas kernels: 124 us -> 116 us  [body(): pl.pallas_call(functools.partial(kernel, sizes), out_shape=pltpu.VMEM((2,...]
where the time goes in v4:
time: 117 us
  Pallas kernels  116 us (99%)
    pallas_call x1, Pallas kernels, body(): pl.pallas_call(functools.partial(kernel, sizes), out_shape=pltpu.VMEM((2,...  116 us

profile of v4, /device:TPU:513, one launch (start us, length us, event | category | flops | bytes accessed | tf_op | source)
XLA Modules:
  0.0 116.6 jit_solution(10192551016111569527)
XLA Ops:
  0.0 115.8 %shard_map.109 = f32[2,16,2048]{2,1,0:T(8,128)S(1)} custom-call(s32[6]{0:T(128)} %cuts_hbm.1, f32[3,16,2048]{2,1,0:T(8,128)} %sky_hbm.1, f32[3,256,128]{2,1,0:T(8,128)} %bitcast.15, f32[2,256,128]{2,1,0:T(8,128)} %bitcast.16, f32[1,256,128]{2,1,0:T(8,128)} %bitcast.17, bf16[2,512,512]{2,1,0:T(8,128)(2,1)} %constant.12.clone.fwd_rows_hbm, ...), custom_call_target="tpu_custom_call" | custom-call | tf_op jit(solution)/shard_map/pallas_call | solution.py:464
  115.8 0.7 copy.16

commit v5 on v4

--- a/solution.py
+++ b/solution.py
@@ -370,25 +370,28 @@
 
     arrive(3, both, 6)
     arrive(4, both, 7)
-    products = []
     for h in range(local):
         a_real, a_imag = to_maps(3, h)
         g_real, g_imag = to_maps(4, h)
-        products.append((a_real * g_real - a_imag * g_imag, a_real * g_imag + a_imag * g_real))
-    for h in range(local):
-        c_real, c_imag = products[h]
+        result[h, :, :share] = a_real * g_real - a_imag * g_imag
+        result[h, :, share : 2 * share] = a_real * g_imag + a_imag * g_real
+
+    def current_part(h, carry):
         arrive(pair, h, sem_of(5, h))
         p_real, p_imag = to_maps(5, h)
         x_real, x_imag = to_maps(6, h)
-        c_real = c_real + (p_real * x_real + p_imag * x_imag)
+        c_real = result[h, :, :share] + (p_real * x_real + p_imag * x_imag)
         arrive(7, h, sem_of(7, h))
         y_real, y_imag = to_maps(7, h)
-        c_imag = c_imag - (p_real * y_imag - p_imag * y_real)
+        c_imag = result[h, :, share : 2 * share] - (p_real * y_imag - p_imag * y_real)
         spectra = table_dot(fwd_rows, jnp.concatenate([c_real, c_imag], axis=0))
         sent[8, h] = jnp.concatenate(
             [spectra[j * span : (j + 1) * span] for j in range(local)], axis=1
         )
         exchange(8, h, sem_of(8, h))
+        return carry
+
+    lax.fori_loop(0, local, current_part, 0)
     mixed = []
     for h in range(local):
         arrive(8, h, sem_of(8, h))
@@ -399,13 +402,13 @@
     for h in range(local):
         exchange(9, h, sem_of(9, h))
     last = 8 + 4 * local
-    for h in range(local):
+    def estimate_part(h, done):
         arrive(9, h, sem_of(9, h))
         e_real, e_imag = to_maps(9, h)
         result[h, :, :share] = e_real
         result[h, :, share : 2 * share] = e_imag
 
-        def gather(step, carry, h=h):
+        def gather(step, carry):
             row = far_row(step)
             pltpu.make_async_remote_copy(
                 src_ref=result.at[h, pl.ds(row * slab, slab), :],
@@ -423,6 +426,9 @@
             stage.at[h, pl.ds(row_me * slab, slab), :],
             recv_sems.at[last + h],
         ).start()
+        return done
+
+    lax.fori_loop(0, local, estimate_part, 0)
     for h in range(local):
         pltpu.make_async_copy(stage.at[h], stage.at[h], recv_sems.at[last + h]).wait()
     for row in range(n_rows):

time: 117 us -> 117 us (level)
  no operation moved by 1% of the time
where the time goes in v5:
time: 117 us; the launch traced here: 116 us
  Pallas kernels  116 us (99%)
    pallas_call x1, Pallas kernels, body(): pl.pallas_call(functools.partial(kernel, sizes), out_shape=pltpu.VMEM((2,...  116 us

profile of v5, /device:TPU:513, one launch (start us, length us, event | category | flops | bytes accessed | tf_op | source)
XLA Modules:
  0.0 116.4 jit_solution(18425116140995168621)
XLA Ops:
  0.0 115.7 %shard_map.109 = f32[2,16,2048]{2,1,0:T(8,128)S(1)} custom-call(s32[6]{0:T(128)} %cuts_hbm.1, f32[3,16,2048]{2,1,0:T(8,128)} %sky_hbm.1, f32[3,256,128]{2,1,0:T(8,128)} %bitcast.15, f32[2,256,128]{2,1,0:T(8,128)} %bitcast.16, f32[1,256,128]{2,1,0:T(8,128)} %bitcast.17, bf16[2,512,512]{2,1,0:T(8,128)(2,1)} %constant.12.clone.fwd_rows_hbm, ...), custom_call_target="tpu_custom_call" | custom-call | tf_op jit(solution)/shard_map/pallas_call | solution.py:470
  115.7 0.7 copy.16
